TPU v7x, 128 devices: a whole 4x4x4 slice. The times are simulated.
128 devices in a mesh: depth: 4 (over x_lo, core), lat: 32 (over z, x_hi, y).
Axes of the slice: x: 4 (x_hi: 2, x_lo: 2; x = x_hi * 2 + x_lo), y: 4, z: 4, core: 2. Of those that a mesh axis runs over, the one named last changes fastest.
Arguments:
- source: float32 [4, 2, 320, 128, 512], P(None, None, 'depth', 'lat'), may hold values from -6 to 6
- line_inverse: float32 [4, 2, 80, 80], P('depth'), may hold values from -0.6 to 1.6, as said below
- plane_count: int32 [4], P('depth'), may hold values from 48 to 80
- classes: int32 [320, 128, 512], P('depth', 'lat'), may hold values from 0 to 15
- table_re: float32 [16], replicated, may hold values from -2 to 2
- table_im: float32 [16], replicated, may hold values from 0.5 to 2
Outputs:
- field: float32 [4, 2, 320, 128, 512], P(None, None, 'depth', 'lat')
Inputs may be any that keep to these rules, and one draw needn't show every extreme that they name: `line_inverse`: a dense complex matrix for each layer whose real diagonal is about 0.8.
All inputs are finite; a program needn't handle non-finite values.
Results may differ from a plain program's by a relative error of at most 0.0001.
Values sent between devices are 32-bit elements; how exact they have to be, the bound alone decides.
A program may use at most 128 MiB of HBM per device.

v0:
```python
import functools

import jax
import jax.numpy as jnp
from jax import lax
from jax.experimental import pallas as pl
from jax.experimental.pallas import tpu as pltpu
from jax.sharding import PartitionSpec as P

MESH = pl.DeviceIdType.MESH
CLASSES = 16
CORRECTION = 0.1
NEAR = 4.0 / 3.0
FAR = -1.0 / 12.0
BLOCK = 16
EXTRA = 16
PIECES_FIRST = 2
PIECES_BASE_OUTER = 1
PIECES_BASE_INNER = 2
PIECES_TRACE = 1


def along_y(x):
    size = x.shape[1]
    lane = lax.broadcasted_iota(jnp.int32, x.shape, 1)
    near = jnp.where(lane >= 1, pltpu.roll(x, 1, 1), 0.0) + jnp.where(
        lane < size - 1, pltpu.roll(x, size - 1, 1), 0.0
    )
    far = jnp.where(lane >= 2, pltpu.roll(x, 2, 1), 0.0) + jnp.where(
        lane < size - 2, pltpu.roll(x, size - 2, 1), 0.0
    )
    return NEAR * near + FAR * far


def field_kernel(
    source, matrix, count, classes, table_re, table_im, field,
    held, cells, solved, halo, kappa, plane, base, inbound, outbound, spread, column, coeff, weights,
    load_sem, cell_sem, bulk_send, bulk_recv, base_send, base_recv, trace_send, trace_recv,
):
    shots, rows, _, planes, width = held.shape
    half = shots // 2
    pieces = shots * 4
    d = lax.axis_index("depth")
    l = lax.axis_index("lat")
    layers = lax.axis_size("depth")
    tiles = lax.axis_size("lat")
    has_prev = l > 0
    has_next = l < tiles - 1
    inner = (d > 0) & (d < layers - 1)
    last = count[0] - 1

    def load(s, r):
        return pltpu.make_async_copy(source.at[s, :, :, r, :], held.at[s, r], load_sem.at[s, r])

    def load_cells(r):
        return pltpu.make_async_copy(classes.at[:, r, :], cells.at[r], cell_sem.at[r])

    for r in (0, 3, 1, 2):
        load(0, r).start()
    for s in range(1, shots):
        for r in range(rows):
            load(s, r).start()
    for r in range(rows):
        load_cells(r).start()

    base[...] = jnp.zeros_like(base)
    inbound[...] = jnp.zeros_like(inbound)

    barrier = pltpu.get_barrier_semaphore()
    expected = 0
    for by_d in (-1, 0, 1):
        for by_l in (-1, 0, 1):
            if by_d == 0 and by_l == 0:
                continue
            there = (d + by_d >= 0) & (d + by_d < layers) & (l + by_l >= 0) & (l + by_l < tiles)
            expected = expected + jnp.where(there, 1, 0)

            @pl.when(there)
            def _():
                pl.semaphore_signal(barrier, inc=1, device_id=(d + by_d, l + by_l), device_id_type=MESH)

    at_row = lax.broadcasted_iota(jnp.int32, (planes, planes), 0)
    at_column = lax.broadcasted_iota(jnp.int32, (planes, planes), 1)
    live = (at_row <= last) & (at_column <= last)
    real = jnp.where(live, matrix[0, 0], 0.0)
    imag = jnp.where(live, matrix[0, 1], 0.0)
    end_re = jnp.sum(jnp.where(at_row == last, real, 0.0), axis=0, keepdims=True)
    end_im = jnp.sum(jnp.where(at_row == last, imag, 0.0), axis=0, keepdims=True)
    whole = jnp.concatenate(
        [
            jnp.concatenate([real, -imag], axis=1),
            jnp.concatenate([imag, real], axis=1),
            jnp.concatenate(
                [
                    jnp.concatenate([end_re, -end_im], axis=1),
                    jnp.concatenate([end_im, end_re], axis=1),
                    jnp.concatenate([real[:1], -imag[:1]], axis=1),
                    jnp.concatenate([imag[:1], real[:1]], axis=1),
                    jnp.zeros((EXTRA - 4, 2 * planes), jnp.float32),
                ],
                axis=0,
            ),
        ],
        axis=0,
    )
    high = whole.astype(jnp.bfloat16)
    low = (whole - high.astype(jnp.float32)).astype(jnp.bfloat16)
    tall = 2 * planes + EXTRA
    weights[:tall] = high
    weights[tall:] = low
    for side, pick in ((0, at_column == 0), (1, at_column == last)):
        for part, values in ((0, real), (1, imag)):
            picked = jnp.sum(jnp.where(pick, values, 0.0), axis=1, keepdims=True)
            column[side, part] = jnp.broadcast_to(picked, (planes, 128))
    for part, values in ((0, real), (1, imag)):
        for side, pick in ((0, (at_row == last) & (at_column == 0)), (1, (at_row == 0) & (at_column == last))):
            picked = jnp.sum(jnp.sum(jnp.where(pick, values, 0.0), axis=1, keepdims=True), axis=0, keepdims=True)
            coeff[side, part] = jnp.broadcast_to(picked, (half, 128))

    def solve(s, r):
        load(s, r).wait()
        values = held[s, r].reshape(2 * planes, width)
        upper = values.astype(jnp.bfloat16)
        lower = (values - upper.astype(jnp.float32)).astype(jnp.bfloat16)
        first = jnp.dot(weights[...], upper, preferred_element_type=jnp.float32)
        second = jnp.dot(weights[:tall], lower, preferred_element_type=jnp.float32)
        total = first[:tall] + first[tall:] + second
        solved[s, r] = total[: 2 * planes].reshape(2, planes, width)
        side = s // half
        for part in range(2):
            row = jnp.where(
                side == 0,
                total[2 * planes + part : 2 * planes + part + 1],
                total[2 * planes + 2 + part : 2 * planes + 3 + part],
            )
            base[side, part, r + 2, pl.ds(s % half, 1), :] = row

    def piece(k, to_next):
        s, a, part = k // 4, (k % 4) // 2, k % 2
        if to_next:
            return pltpu.make_async_remote_copy(
                src_ref=solved.at[s, 3 - a, part],
                dst_ref=halo.at[s, 1 - a, part],
                send_sem=bulk_send.at[1, k],
                recv_sem=bulk_recv.at[1, k],
                device_id=(d, l + 1),
                device_id_type=MESH,
            )
        return pltpu.make_async_remote_copy(
            src_ref=solved.at[s, a, part],
            dst_ref=halo.at[s, 2 + a, part],
            send_sem=bulk_send.at[0, k],
            recv_sem=bulk_recv.at[0, k],
            device_id=(d, l - 1),
            device_id_type=MESH,
        )

    def send_pieces(start, stop):
        for to_next, there in ((False, has_prev), (True, has_next)):

            @pl.when(there)
            def _():
                def step(k, carry):
                    piece(k, to_next).start()
                    return carry

                lax.fori_loop(start, stop, step, 0)

    solve(0, 0)
    solve(0, 3)
    pl.semaphore_wait(barrier, expected)
    send_pieces(0, PIECES_FIRST)
    solve(0, 1)
    solve(0, 2)

    def solve_shot(s, carry):
        for r in range(rows):
            solve(s, r)
        return carry

    lax.fori_loop(1, shots, solve_shot, 0)

    def base_copy(to_next):
        if to_next:
            return pltpu.make_async_remote_copy(
                src_ref=base.at[:, :, pl.ds(4, 2)],
                dst_ref=base.at[:, :, pl.ds(0, 2)],
                send_sem=base_send.at[1],
                recv_sem=base_recv.at[1],
                device_id=(d, l + 1),
                device_id_type=MESH,
            )
        return pltpu.make_async_remote_copy(
            src_ref=base.at[:, :, pl.ds(2, 2)],
            dst_ref=base.at[:, :, pl.ds(6, 2)],
            send_sem=base_send.at[0],
            recv_sem=base_recv.at[0],
            device_id=(d, l - 1),
            device_id_type=MESH,
        )

    for to_next, there in ((False, has_prev), (True, has_next)):

        @pl.when(there)
        def _():
            base_copy(to_next).start()

    @pl.when(inner)
    def _():
        send_pieces(PIECES_FIRST, PIECES_FIRST + PIECES_BASE_INNER)

    @pl.when(jnp.logical_not(inner))
    def _():
        send_pieces(PIECES_FIRST, PIECES_FIRST + PIECES_BASE_OUTER)

    for r in range(rows):
        load_cells(r).wait()

        def look_up(i, carry):
            at = pl.ds(pl.multiple_of(i * BLOCK, BLOCK), BLOCK)
            kinds = cells[r, at, :]
            re = jnp.full(kinds.shape, table_re[0], jnp.float32)
            im = jnp.full(kinds.shape, table_im[0], jnp.float32)
            for kind in range(1, CLASSES):
                hit = kinds == kind
                re = jnp.where(hit, table_re[kind], re)
                im = jnp.where(hit, table_im[kind], im)
            kappa[r, 0, at, :] = re
            kappa[r, 1, at, :] = im
            bottom = lax.broadcasted_iota(jnp.int32, kinds.shape, 0) + i * BLOCK == last
            return (carry[0] + jnp.where(bottom, re, 0.0), carry[1] + jnp.where(bottom, im, 0.0))

        zeros = jnp.zeros((BLOCK, width), jnp.float32)
        sums = lax.fori_loop(0, planes // BLOCK, look_up, (zeros, zeros))
        for part in range(2):
            plane[0, part, r] = jnp.broadcast_to(jnp.sum(sums[part], axis=0, keepdims=True), (half, width))
            plane[1, part, r] = jnp.broadcast_to(kappa[r, part, pl.ds(0, 1), :], (half, width))

    @pl.when(has_prev)
    def _():
        base_copy(True).wait_recv()

    @pl.when(has_next)
    def _():
        base_copy(False).wait_recv()

    def lateral(values, r):
        at = r + 2
        return (
            NEAR * (values[at - 1] + values[at + 1])
            + FAR * (values[at - 2] + values[at + 2])
            + along_y(values[at])
            - 5.0 * values[at]
        )

    def trace_copies(side):
        to = d + 1 - 2 * side
        return (
            (
                True,
                True,
                lambda: pltpu.make_async_remote_copy(
                    src_ref=outbound.at[side],
                    dst_ref=inbound.at[side, :, pl.ds(2, 4)],
                    send_sem=trace_send.at[side, 0],
                    recv_sem=trace_recv.at[side, 0],
                    device_id=(to, l),
                    device_id_type=MESH,
                ),
            ),
            (
                has_prev,
                has_next,
                lambda: pltpu.make_async_remote_copy(
                    src_ref=outbound.at[side, :, pl.ds(0, 2)],
                    dst_ref=inbound.at[side, :, pl.ds(6, 2)],
                    send_sem=trace_send.at[side, 1],
                    recv_sem=trace_recv.at[side, 1],
                    device_id=(to, l - 1),
                    device_id_type=MESH,
                ),
            ),
            (
                has_next,
                has_prev,
                lambda: pltpu.make_async_remote_copy(
                    src_ref=outbound.at[side, :, pl.ds(2, 2)],
                    dst_ref=inbound.at[side, :, pl.ds(0, 2)],
                    send_sem=trace_send.at[side, 2],
                    recv_sem=trace_recv.at[side, 2],
                    device_id=(to, l + 1),
                    device_id_type=MESH,
                ),
            ),
        )

    def under(there, act):
        if there is True:
            act()
        else:
            pl.when(there)(act)

    def emit(side):
        factor = [
            jnp.concatenate([coeff[side, part]] * (width // 128), axis=1) for part in range(2)
        ]
        planar = ([], [])
        for row in range(rows + 4):
            t_re, t_im = inbound[side, 0, row], inbound[side, 1, row]
            planar[0].append(base[side, 0, row] + factor[0] * t_re - factor[1] * t_im)
            planar[1].append(base[side, 1, row] + factor[0] * t_im + factor[1] * t_re)
        for r in range(rows):
            re, im = planar[0][r + 2], planar[1][r + 2]
            k_re, k_im = plane[side, 0, r], plane[side, 1, r]
            outbound[side, 0, r] = re + CORRECTION * (lateral(planar[0], r) + k_re * re - k_im * im)
            outbound[side, 1, r] = im + CORRECTION * (lateral(planar[1], r) + k_re * im + k_im * re)
        for goes, _, copy in trace_copies(side):
            under(goes, lambda: copy().start())

    def take(side):
        for _, comes, copy in trace_copies(side):
            under(comes, lambda: copy().wait_recv())

    side_one = jnp.where(d >= layers // 2, 1, 0)
    side_two = 1 - side_one

    @pl.when(inner)
    def _():
        take(side_one)

    emit(side_one)
    sent_inner = PIECES_FIRST + PIECES_BASE_INNER

    @pl.when(inner)
    def _():
        send_pieces(sent_inner, sent_inner + PIECES_TRACE)

    @pl.when(jnp.logical_not(inner))
    def _():
        send_pieces(PIECES_FIRST + PIECES_BASE_OUTER, pieces)

    take(side_two)

    @pl.when(inner)
    def _():
        emit(side_two)
        send_pieces(sent_inner + PIECES_TRACE, pieces)

    for side in range(2):
        for part in range(2):
            values = [inbound[side, part, row] for row in range(rows + 4)]
            for r in range(rows):
                spread[side, part, r] = values[r + 2] + CORRECTION * lateral(values, r)

    def own_rows(s, carry):
        side, shot = s // half, s % half
        for r in range(rows):
            t = [inbound[side, part, r + 2, pl.ds(shot, 1), :] for part in range(2)]
            e = [spread[side, part, r, pl.ds(shot, 1), :] for part in range(2)]

            def block(i, inside):
                at = pl.ds(pl.multiple_of(i * BLOCK, BLOCK), BLOCK)
                g_re, g_im = (
                    jnp.concatenate([column[side, part, at, :]] * (width // 128), axis=1) for part in range(2)
                )
                linear, values = [], []
                for part in range(2):
                    v = solved[s, r, part, at, :]
                    near = [solved[s, q, part, at, :] for q in (r - 1, r + 1) if 0 <= q < rows]
                    far = [solved[s, q, part, at, :] for q in (r - 2, r + 2) if 0 <= q < rows]
                    total = along_y(v) - 5.0 * v + NEAR * sum(near[1:], near[0]) + FAR * sum(far[1:], far[0])
                    linear.append(v + CORRECTION * total)
                    values.append(v)
                v_re = values[0] + g_re * t[0] - g_im * t[1]
                v_im = values[1] + g_re * t[1] + g_im * t[0]
                k_re, k_im = kappa[r, 0, at, :], kappa[r, 1, at, :]
                field[s, r, 0, at, :] = (
                    linear[0] + g_re * e[0] - g_im * e[1] + CORRECTION * (k_re * v_re - k_im * v_im)
                )
                field[s, r, 1, at, :] = (
                    linear[1] + g_re * e[1] + g_im * e[0] + CORRECTION * (k_re * v_im + k_im * v_re)
                )
                return inside

            lax.fori_loop(0, planes // BLOCK, block, 0)
        return carry

    lax.fori_loop(0, shots, own_rows, 0)

    def add_rows(s, part, q, to_rows):
        def block(i, inside):
            at = pl.ds(pl.multiple_of(i * BLOCK, BLOCK), BLOCK)
            v = halo[s, q, part, at, :]
            for r, weight in to_rows:
                field[s, r, part, at, :] = field[s, r, part, at, :] + (CORRECTION * weight) * v
            return inside

        lax.fori_loop(0, planes // BLOCK, block, 0)

    def add_shot(s, carry):
        for a in range(2):
            for part in range(2):
                k = s * 4 + a * 2 + part

                @pl.when(has_next)
                def _():
                    piece(k, False).wait_recv()
                    add_rows(s, part, 2 + a, ((3, NEAR), (2, FAR)) if a == 0 else ((3, FAR),))

                @pl.when(has_prev)
                def _():
                    piece(k, True).wait_recv()
                    add_rows(s, part, 1 - a, ((0, NEAR), (1, FAR)) if a == 0 else ((0, FAR),))
        return carry

    lax.fori_loop(0, shots, add_shot, 0)

    for to_next, there in ((False, has_prev), (True, has_next)):

        @pl.when(there)
        def _():
            base_copy(to_next).wait_send()

            def step(k, carry):
                piece(k, to_next).wait_send()
                return carry

            lax.fori_loop(0, pieces, step, 0)

    for goes, _, copy in trace_copies(side_one):
        under(goes, lambda: copy().wait_send())

    @pl.when(inner)
    def _():
        for goes, _, copy in trace_copies(side_two):
            under(goes, lambda: copy().wait_send())


def write_kernel(field, out, sem):
    shots, rows = field.shape[:2]

    def copy(s, r):
        return pltpu.make_async_copy(field.at[s, r], out.at[s, :, :, r, :], sem.at[s, r])

    for s in range(shots):
        for r in range(rows):
            copy(s, r).start()
    for s in range(shots):
        for r in range(rows):
            copy(s, r).wait()


def on_device(source, line_inverse, plane_count, classes, table_re, table_im):
    shots, parts, planes, rows, width = source.shape
    half = shots // 2
    by_rows = (shots, rows, parts, planes, width)
    any_space = pl.BlockSpec(memory_space=pl.ANY)
    vmem = pl.BlockSpec(memory_space=pltpu.VMEM)
    smem = pl.BlockSpec(memory_space=pltpu.SMEM)
    tall = 2 * planes + EXTRA
    pieces = shots * 4
    dma = pltpu.SemaphoreType.DMA
    field = pl.pallas_call(
        field_kernel,
        out_shape=jax.ShapeDtypeStruct(by_rows, jnp.float32),
        in_specs=[any_space, vmem, smem, any_space, smem, smem],
        out_specs=vmem,
        scratch_shapes=[
            pltpu.VMEM(by_rows, jnp.float32),
            pltpu.VMEM((rows, planes, width), jnp.int32),
            pltpu.VMEM(by_rows, jnp.float32),
            pltpu.VMEM((shots, 4, parts, planes, width), jnp.float32),
            pltpu.VMEM((rows, parts, planes, width), jnp.float32),
            pltpu.VMEM((2, parts, rows, half, width), jnp.float32),
            pltpu.VMEM((2, parts, rows + 4, half, width), jnp.float32),
            pltpu.VMEM((2, parts, rows + 4, half, width), jnp.float32),
            pltpu.VMEM((2, parts, rows, half, width), jnp.float32),
            pltpu.VMEM((2, parts, rows, half, width), jnp.float32),
            pltpu.VMEM((2, parts, planes, 128), jnp.float32),
            pltpu.VMEM((2, parts, half, 128), jnp.float32),
            pltpu.VMEM((2 * tall, 2 * planes), jnp.bfloat16),
            dma((shots, rows)),
            dma((rows,)),
            dma((2, pieces)),
            dma((2, pieces)),
            dma((2,)),
            dma((2,)),
            dma((2, 3)),
            dma((2, 3)),
        ],
        compiler_params=pltpu.CompilerParams(
            collective_id=0, has_side_effects=True, vmem_limit_bytes=56 * 2**20
        ),
    )(source, line_inverse, plane_count, classes, table_re, table_im)
    return pl.pallas_call(
        write_kernel,
        out_shape=jax.ShapeDtypeStruct(source.shape, jnp.float32),
        in_specs=[vmem],
        out_specs=any_space,
        scratch_shapes=[dma((shots, rows))],
        compiler_params=pltpu.CompilerParams(vmem_limit_bytes=8 * 2**20),
    )(field)


def solution(mesh):
    in_specs = (
        P(None, None, "depth", "lat", None),
        P("depth", None, None, None),
        P("depth"),
        P("depth", "lat", None),
        P(),
        P(),
    )
    out_specs = P(None, None, "depth", "lat", None)
    return jax.shard_map(
        on_device, mesh=mesh, in_specs=in_specs, out_specs=out_specs, check_vma=False
    )
```

profile of v0, /device:TPU:97, one launch (start us, length us, event | category | flops | bytes accessed | tf_op | source)
XLA Modules:
  0.0 78.0 jit_solution(203369464871902402)
XLA Ops:
  0.7 72.4 %shard_map.64.field = f32[4,4,2,80,512]{4,3,2,1,0:T(8,128)} custom-call(f32[4,2,80,4,512]{4,3,2,1,0:T(4,128)} %source.1, f32[1,2,80,80]{3,2,1,0:T(8,128)} %matrix.1, s32[1]{0:T(128)S(6)} %copy.7.count, s32[80,4,512]{2,1,0:T(4,128)} %classes.1, f32[16]{0:T(128)} %table_re.1, f32[16]{0:T(128)} %table_im.1), custom_call_target="tpu_custom_call" | custom-call | tf_op jit(solution)/shard_map/pallas_call | solution.py:463
  73.1 0.0 copy-start
  73.1 2.5 %copy-done = f32[4,4,2,80,512]{4,3,2,1,0:T(8,128)S(1)} copy-done((f32[4,4,2,80,512]{4,3,2,1,0:T(8,128)S(1)}, f32[4,4,2,80,512]{4,3,2,1,0:T(8,128)}, u32[]{:S(2)}) %copy-start) | copy-done | bytes 5242904
  75.5 2.5 %shard_map.65 = f32[4,2,80,4,512]{4,3,2,1,0:T(4,128)} custom-call(f32[4,4,2,80,512]{4,3,2,1,0:T(8,128)S(1)} %copy-done), custom_call_target="tpu_custom_call" | custom-call | tf_op jit(solution)/shard_map/pallas_call | solution.py:495
Async XLA Ops:
  73.1 2.5 %copy-start = (f32[4,4,2,80,512]{4,3,2,1,0:T(8,128)S(1)}, f32[4,4,2,80,512]{4,3,2,1,0:T(8,128)}, u32[]{:S(2)}) copy-start(f32[4,4,2,80,512]{4,3,2,1,0:T(8,128)} %shard_map.64.field) | copy-start | bytes 15728644
where the time goes:
time: 78.2 us; the launch traced here: 78 us
  Pallas kernels  74.9 us (96%)
  local copies, waits for them, and re-layouts  2.48 us (3%)
    pallas_call x1, Pallas kernels, on_device(): pl.pallas_call(field_kernel, out_shape=jax.ShapeDtypeStruct(by_rows, jnp....  72.4 us
    unnamed x2, local copies, waits for them, and re-layouts  2.48 us
    pallas_call x1, Pallas kernels, on_device(): pl.pallas_call(write_kernel, out_shape=jax.ShapeDtypeStruct(source.shape,...  2.46 us

commit v1 on v0

--- a/solution.py
+++ b/solution.py
@@ -33,9 +33,10 @@
 
 
 def field_kernel(
-    source, matrix, count, classes, table_re, table_im, field,
+    count, source, matrix_from, classes, table_re_from, table_im_from, field,
+    matrix, table_re, table_im,
     held, cells, solved, halo, kappa, plane, base, inbound, outbound, spread, column, coeff, weights,
-    load_sem, cell_sem, bulk_send, bulk_recv, base_send, base_recv, trace_send, trace_recv,
+    small_sem, load_sem, cell_sem, bulk_send, bulk_recv, base_send, base_recv, trace_send, trace_recv,
 ):
     shots, rows, _, planes, width = held.shape
     half = shots // 2
@@ -47,7 +48,6 @@
     has_prev = l > 0
     has_next = l < tiles - 1
     inner = (d > 0) & (d < layers - 1)
-    last = count[0] - 1
 
     def load(s, r):
         return pltpu.make_async_copy(source.at[s, :, :, r, :], held.at[s, r], load_sem.at[s, r])
@@ -55,8 +55,17 @@
     def load_cells(r):
         return pltpu.make_async_copy(classes.at[:, r, :], cells.at[r], cell_sem.at[r])
 
+    small = [
+        pltpu.make_async_copy(here, there, small_sem.at[i])
+        for i, (here, there) in enumerate(
+            ((matrix_from.at[0], matrix), (table_re_from, table_re), (table_im_from, table_im))
+        )
+    ]
+    small[0].start()
     for r in (0, 3, 1, 2):
         load(0, r).start()
+    small[1].start()
+    small[2].start()
     for s in range(1, shots):
         for r in range(rows):
             load(s, r).start()
@@ -79,11 +88,13 @@
             def _():
                 pl.semaphore_signal(barrier, inc=1, device_id=(d + by_d, l + by_l), device_id_type=MESH)
 
+    small[0].wait()
+    last = count[0] - 1
     at_row = lax.broadcasted_iota(jnp.int32, (planes, planes), 0)
     at_column = lax.broadcasted_iota(jnp.int32, (planes, planes), 1)
     live = (at_row <= last) & (at_column <= last)
-    real = jnp.where(live, matrix[0, 0], 0.0)
-    imag = jnp.where(live, matrix[0, 1], 0.0)
+    real = jnp.where(live, matrix[0], 0.0)
+    imag = jnp.where(live, matrix[1], 0.0)
     end_re = jnp.sum(jnp.where(at_row == last, real, 0.0), axis=0, keepdims=True)
     end_im = jnp.sum(jnp.where(at_row == last, imag, 0.0), axis=0, keepdims=True)
     whole = jnp.concatenate(
@@ -213,6 +224,8 @@
     def _():
         send_pieces(PIECES_FIRST, PIECES_FIRST + PIECES_BASE_OUTER)
 
+    small[1].wait()
+    small[2].wait()
     for r in range(rows):
         load_cells(r).wait()
 
@@ -455,17 +468,21 @@
     half = shots // 2
     by_rows = (shots, rows, parts, planes, width)
     any_space = pl.BlockSpec(memory_space=pl.ANY)
+    hbm = pl.BlockSpec(memory_space=pltpu.HBM)
     vmem = pl.BlockSpec(memory_space=pltpu.VMEM)
-    smem = pl.BlockSpec(memory_space=pltpu.SMEM)
     tall = 2 * planes + EXTRA
     pieces = shots * 4
     dma = pltpu.SemaphoreType.DMA
+    operands = (source, line_inverse, classes, table_re, table_im)
     field = pl.pallas_call(
         field_kernel,
         out_shape=jax.ShapeDtypeStruct(by_rows, jnp.float32),
-        in_specs=[any_space, vmem, smem, any_space, smem, smem],
+        in_specs=[pl.BlockSpec(memory_space=pltpu.SMEM)] + [hbm] * len(operands),
         out_specs=vmem,
         scratch_shapes=[
+            pltpu.VMEM((parts, planes, planes), jnp.float32),
+            pltpu.SMEM((CLASSES,), jnp.float32),
+            pltpu.SMEM((CLASSES,), jnp.float32),
             pltpu.VMEM(by_rows, jnp.float32),
             pltpu.VMEM((rows, planes, width), jnp.int32),
             pltpu.VMEM(by_rows, jnp.float32),
@@ -479,6 +496,7 @@
             pltpu.VMEM((2, parts, planes, 128), jnp.float32),
             pltpu.VMEM((2, parts, half, 128), jnp.float32),
             pltpu.VMEM((2 * tall, 2 * planes), jnp.bfloat16),
+            dma((3,)),
             dma((shots, rows)),
             dma((rows,)),
             dma((2, pieces)),
@@ -489,9 +507,9 @@
             dma((2, 3)),
         ],
         compiler_params=pltpu.CompilerParams(
-            collective_id=0, has_side_effects=True, vmem_limit_bytes=56 * 2**20
+            collective_id=0, has_side_effects=True, vmem_limit_bytes=40 * 2**20
         ),
-    )(source, line_inverse, plane_count, classes, table_re, table_im)
+    )(plane_count, *(pltpu.with_memory_space_constraint(x, pltpu.HBM) for x in operands))
     return pl.pallas_call(
         write_kernel,
         out_shape=jax.ShapeDtypeStruct(source.shape, jnp.float32),

time: 78.2 us -> 72.5 us (0.927)
  Pallas kernels: 74.9 us -> 71.7 us
  local copies, waits for them, and re-layouts: 2.48 us -> 0 us
    pallas_call x1, Pallas kernels: 72.4 us -> 69.2 us  [on_device(): pl.pallas_call(field_kernel, out_shape=jax.ShapeDtypeStruct(by_rows, jnp....]
    unnamed x2 -> x0, local copies, waits for them, and re-layouts: 2.48 us -> none
where the time goes in v1:
time: 72.5 us; the launch traced here: 72.3 us
  Pallas kernels  71.7 us (99%)
    pallas_call x1, Pallas kernels, on_device(): pl.pallas_call(field_kernel, out_shape=jax.ShapeDtypeStruct(by_rows, jnp....  69.2 us
    pallas_call x1, Pallas kernels, on_device(): pl.pallas_call(write_kernel, out_shape=jax.ShapeDtypeStruct(source.shape,...  2.46 us

profile of v1, /device:TPU:97, one launch (start us, length us, event | category | flops | bytes accessed | tf_op | source)
XLA Modules:
  0.0 72.3 jit_solution(13098939300592925251)
XLA Ops:
  0.7 69.2 %shard_map.64.field = f32[4,4,2,80,512]{4,3,2,1,0:T(8,128)S(1)} custom-call(s32[1]{0:T(128)S(6)} %copy.7.count, f32[4,2,80,4,512]{4,3,2,1,0:T(4,128)} %source.1, f32[1,2,80,80]{3,2,1,0:T(8,128)} %matrix_from.1, s32[80,4,512]{2,1,0:T(4,128)} %classes.1, f32[16]{0:T(128)} %table_re_from.1, f32[16]{0:T(128)} %table_im_from.1), custom_call_target="tpu_custom_call" | custom-call | tf_op jit(solution)/shard_map/pallas_call | solution.py:477
  69.9 2.5 %shard_map.65 = f32[4,2,80,4,512]{4,3,2,1,0:T(4,128)} custom-call(f32[4,4,2,80,512]{4,3,2,1,0:T(8,128)S(1)} %shard_map.64.field), custom_call_target="tpu_custom_call" | custom-call | tf_op jit(solution)/shard_map/pallas_call | solution.py:513

commit v2 on v1

--- a/solution.py
+++ b/solution.py
@@ -15,9 +15,10 @@
 BLOCK = 16
 EXTRA = 16
 PIECES_FIRST = 2
-PIECES_BASE_OUTER = 1
-PIECES_BASE_INNER = 2
-PIECES_TRACE = 1
+PIECES_SOLVE = 3
+PIECES_BASE_OUTER = 2
+PIECES_BASE_INNER = 4
+PIECES_TRACE = 3
 
 
 def along_y(x):
@@ -37,6 +38,7 @@
     matrix, table_re, table_im,
     held, cells, solved, halo, kappa, plane, base, inbound, outbound, spread, column, coeff, weights,
     small_sem, load_sem, cell_sem, bulk_send, bulk_recv, base_send, base_recv, trace_send, trace_recv,
+    ready_sem,
 ):
     shots, rows, _, planes, width = held.shape
     half = shots // 2
@@ -47,7 +49,11 @@
     tiles = lax.axis_size("lat")
     has_prev = l > 0
     has_next = l < tiles - 1
-    inner = (d > 0) & (d < layers - 1)
+    has_above = d > 0
+    has_below = d < layers - 1
+    inner = has_above & has_below
+    side_one = jnp.where(d >= layers // 2, 1, 0)
+    side_two = 1 - side_one
 
     def load(s, r):
         return pltpu.make_async_copy(source.at[s, :, :, r, :], held.at[s, r], load_sem.at[s, r])
@@ -61,6 +67,16 @@
             ((matrix_from.at[0], matrix), (table_re_from, table_re), (table_im_from, table_im))
         )
     ]
+    barrier = pltpu.get_barrier_semaphore()
+    beside = ((has_prev, 0, -1), (has_next, 0, 1), (has_above, -1, 0), (has_below, 1, 0))
+    for there, by_d, by_l in beside:
+
+        @pl.when(there)
+        def _():
+            pl.semaphore_signal(barrier, inc=1, device_id=(d + by_d, l + by_l), device_id_type=MESH)
+
+    expected = sum(jnp.where(there, 1, 0) for there, _, _ in beside)
+
     small[0].start()
     for r in (0, 3, 1, 2):
         load(0, r).start()
@@ -72,21 +88,18 @@
     for r in range(rows):
         load_cells(r).start()
 
-    base[...] = jnp.zeros_like(base)
-    inbound[...] = jnp.zeros_like(inbound)
-
-    barrier = pltpu.get_barrier_semaphore()
-    expected = 0
-    for by_d in (-1, 0, 1):
-        for by_l in (-1, 0, 1):
-            if by_d == 0 and by_l == 0:
-                continue
-            there = (d + by_d >= 0) & (d + by_d < layers) & (l + by_l >= 0) & (l + by_l < tiles)
-            expected = expected + jnp.where(there, 1, 0)
-
-            @pl.when(there)
-            def _():
-                pl.semaphore_signal(barrier, inc=1, device_id=(d + by_d, l + by_l), device_id_type=MESH)
+    for there, at in ((has_prev, pl.ds(0, 2)), (has_next, pl.ds(6, 2))):
+
+        @pl.when(jnp.logical_not(there))
+        def _():
+            base[:, :, at] = jnp.zeros((2, 2, 2, half, width), jnp.float32)
+            inbound[:, :, at] = jnp.zeros((2, 2, 2, half, width), jnp.float32)
+
+    for there, side in ((has_above, 0), (has_below, 1)):
+
+        @pl.when(jnp.logical_not(there))
+        def _():
+            inbound[side] = jnp.zeros(inbound.shape[1:], jnp.float32)
 
     small[0].wait()
     last = count[0] - 1
@@ -181,8 +194,15 @@
     solve(0, 3)
     pl.semaphore_wait(barrier, expected)
     send_pieces(0, PIECES_FIRST)
+    for there, by_d in ((has_above, -1), (has_below, 1)):
+
+        @pl.when(there)
+        def _():
+            pl.semaphore_signal(ready_sem, inc=1, device_id=(d + by_d, l), device_id_type=MESH)
+
     solve(0, 1)
     solve(0, 2)
+    send_pieces(PIECES_FIRST, PIECES_SOLVE)
 
     def solve_shot(s, carry):
         for r in range(rows):
@@ -191,38 +211,39 @@
 
     lax.fori_loop(1, shots, solve_shot, 0)
 
-    def base_copy(to_next):
-        if to_next:
-            return pltpu.make_async_remote_copy(
-                src_ref=base.at[:, :, pl.ds(4, 2)],
-                dst_ref=base.at[:, :, pl.ds(0, 2)],
-                send_sem=base_send.at[1],
-                recv_sem=base_recv.at[1],
-                device_id=(d, l + 1),
-                device_id_type=MESH,
-            )
+    def base_copy(side, to_next):
+        source_at, target_at = (4, 0) if to_next else (2, 6)
         return pltpu.make_async_remote_copy(
-            src_ref=base.at[:, :, pl.ds(2, 2)],
-            dst_ref=base.at[:, :, pl.ds(6, 2)],
-            send_sem=base_send.at[0],
-            recv_sem=base_recv.at[0],
-            device_id=(d, l - 1),
+            src_ref=base.at[side, :, pl.ds(source_at, 2)],
+            dst_ref=base.at[side, :, pl.ds(target_at, 2)],
+            send_sem=base_send.at[int(to_next), side],
+            recv_sem=base_recv.at[int(to_next), side],
+            device_id=(d, l + 1 if to_next else l - 1),
             device_id_type=MESH,
         )
 
-    for to_next, there in ((False, has_prev), (True, has_next)):
-
-        @pl.when(there)
-        def _():
-            base_copy(to_next).start()
+    base_copies = tuple(
+        (needed, to_next, side)
+        for needed, side in ((True, side_one), (inner, side_two))
+        for to_next in (False, True)
+    )
+
+    def both(needed, there):
+        return there if needed is True else needed & there
+
+    for needed, to_next, side in base_copies:
+
+        @pl.when(both(needed, has_next if to_next else has_prev))
+        def _():
+            base_copy(side, to_next).start()
 
     @pl.when(inner)
     def _():
-        send_pieces(PIECES_FIRST, PIECES_FIRST + PIECES_BASE_INNER)
+        send_pieces(PIECES_SOLVE, PIECES_SOLVE + PIECES_BASE_INNER)
 
     @pl.when(jnp.logical_not(inner))
     def _():
-        send_pieces(PIECES_FIRST, PIECES_FIRST + PIECES_BASE_OUTER)
+        send_pieces(PIECES_SOLVE, PIECES_SOLVE + PIECES_BASE_OUTER)
 
     small[1].wait()
     small[2].wait()
@@ -249,13 +270,13 @@
             plane[0, part, r] = jnp.broadcast_to(jnp.sum(sums[part], axis=0, keepdims=True), (half, width))
             plane[1, part, r] = jnp.broadcast_to(kappa[r, part, pl.ds(0, 1), :], (half, width))
 
-    @pl.when(has_prev)
-    def _():
-        base_copy(True).wait_recv()
-
-    @pl.when(has_next)
-    def _():
-        base_copy(False).wait_recv()
+    for needed, to_next, side in base_copies:
+
+        @pl.when(both(needed, has_prev if to_next else has_next))
+        def _():
+            base_copy(side, to_next).wait_recv()
+
+    pl.semaphore_wait(ready_sem, jnp.where(has_above, 1, 0) + jnp.where(has_below, 1, 0))
 
     def lateral(values, r):
         at = r + 2
@@ -334,15 +355,12 @@
         for _, comes, copy in trace_copies(side):
             under(comes, lambda: copy().wait_recv())
 
-    side_one = jnp.where(d >= layers // 2, 1, 0)
-    side_two = 1 - side_one
-
     @pl.when(inner)
     def _():
         take(side_one)
 
     emit(side_one)
-    sent_inner = PIECES_FIRST + PIECES_BASE_INNER
+    sent_inner = PIECES_SOLVE + PIECES_BASE_INNER
 
     @pl.when(inner)
     def _():
@@ -350,7 +368,7 @@
 
     @pl.when(jnp.logical_not(inner))
     def _():
-        send_pieces(PIECES_FIRST + PIECES_BASE_OUTER, pieces)
+        send_pieces(PIECES_SOLVE + PIECES_BASE_OUTER, pieces)
 
     take(side_two)
 
@@ -401,14 +419,25 @@
     lax.fori_loop(0, shots, own_rows, 0)
 
     def add_rows(s, part, q, to_rows):
-        def block(i, inside):
-            at = pl.ds(pl.multiple_of(i * BLOCK, BLOCK), BLOCK)
+        for first in range(0, planes, BLOCK):
+            at = pl.ds(first, BLOCK)
             v = halo[s, q, part, at, :]
             for r, weight in to_rows:
                 field[s, r, part, at, :] = field[s, r, part, at, :] + (CORRECTION * weight) * v
-            return inside
-
-        lax.fori_loop(0, planes // BLOCK, block, 0)
+
+    for needed, to_next, side in base_copies:
+
+        @pl.when(both(needed, has_next if to_next else has_prev))
+        def _():
+            base_copy(side, to_next).wait_send()
+
+    for goes, _, copy in trace_copies(side_one):
+        under(goes, lambda: copy().wait_send())
+
+    @pl.when(inner)
+    def _():
+        for goes, _, copy in trace_copies(side_two):
+            under(goes, lambda: copy().wait_send())
 
     def add_shot(s, carry):
         for a in range(2):
@@ -418,35 +447,17 @@
                 @pl.when(has_next)
                 def _():
                     piece(k, False).wait_recv()
+                    piece(k, True).wait_send()
                     add_rows(s, part, 2 + a, ((3, NEAR), (2, FAR)) if a == 0 else ((3, FAR),))
 
                 @pl.when(has_prev)
                 def _():
                     piece(k, True).wait_recv()
+                    piece(k, False).wait_send()
                     add_rows(s, part, 1 - a, ((0, NEAR), (1, FAR)) if a == 0 else ((0, FAR),))
         return carry
 
     lax.fori_loop(0, shots, add_shot, 0)
-
-    for to_next, there in ((False, has_prev), (True, has_next)):
-
-        @pl.when(there)
-        def _():
-            base_copy(to_next).wait_send()
-
-            def step(k, carry):
-                piece(k, to_next).wait_send()
-                return carry
-
-            lax.fori_loop(0, pieces, step, 0)
-
-    for goes, _, copy in trace_copies(side_one):
-        under(goes, lambda: copy().wait_send())
-
-    @pl.when(inner)
-    def _():
-        for goes, _, copy in trace_copies(side_two):
-            under(goes, lambda: copy().wait_send())
 
 
 def write_kernel(field, out, sem):
@@ -501,10 +512,11 @@
             dma((rows,)),
             dma((2, pieces)),
             dma((2, pieces)),
-            dma((2,)),
-            dma((2,)),
+            dma((2, 2)),
+            dma((2, 2)),
             dma((2, 3)),
             dma((2, 3)),
+            pltpu.SemaphoreType.REGULAR,
         ],
         compiler_params=pltpu.CompilerParams(
             collective_id=0, has_side_effects=True, vmem_limit_bytes=40 * 2**20

time: 72.5 us -> 69.8 us (0.963)
  Pallas kernels: 71.7 us -> 69 us
    pallas_call x1, Pallas kernels: 69.2 us -> 66.5 us  [on_device(): pl.pallas_call(field_kernel, out_shape=jax.ShapeDtypeStruct(by_rows, jnp....]
where the time goes in v2:
time: 69.8 us; the launch traced here: 69.7 us
  Pallas kernels  69 us (99%)
    pallas_call x1, Pallas kernels, on_device(): pl.pallas_call(field_kernel, out_shape=jax.ShapeDtypeStruct(by_rows, jnp....  66.5 us
    pallas_call x1, Pallas kernels, on_device(): pl.pallas_call(write_kernel, out_shape=jax.ShapeDtypeStruct(source.shape,...  2.46 us

profile of v2, /device:TPU:97, one launch (start us, length us, event | category | flops | bytes accessed | tf_op | source)
XLA Modules:
  0.0 69.7 jit_solution(4748905347992113404)
XLA Ops:
  0.7 66.5 %shard_map.64.field = f32[4,4,2,80,512]{4,3,2,1,0:T(8,128)S(1)} custom-call(s32[1]{0:T(128)S(6)} %copy.7.count, f32[4,2,80,4,512]{4,3,2,1,0:T(4,128)} %source.1, f32[1,2,80,80]{3,2,1,0:T(8,128)} %matrix_from.1, s32[80,4,512]{2,1,0:T(4,128)} %classes.1, f32[16]{0:T(128)} %table_re_from.1, f32[16]{0:T(128)} %table_im_from.1), custom_call_target="tpu_custom_call" | custom-call | tf_op jit(solution)/shard_map/pallas_call | solution.py:488
  67.2 2.5 %shard_map.65 = f32[4,2,80,4,512]{4,3,2,1,0:T(4,128)} custom-call(f32[4,4,2,80,512]{4,3,2,1,0:T(8,128)S(1)} %shard_map.64.field), custom_call_target="tpu_custom_call" | custom-call | tf_op jit(solution)/shard_map/pallas_call | solution.py:525

commit v3 on v2

--- a/solution.py
+++ b/solution.py
@@ -14,6 +14,9 @@
 FAR = -1.0 / 12.0
 BLOCK = 16
 EXTRA = 16
+RING = 4
+RELAY = 40
+HELD_BACK = 4
 PIECES_FIRST = 2
 PIECES_SOLVE = 3
 PIECES_BASE_OUTER = 2
@@ -38,7 +41,7 @@
     matrix, table_re, table_im,
     held, cells, solved, halo, kappa, plane, base, inbound, outbound, spread, column, coeff, weights,
     small_sem, load_sem, cell_sem, bulk_send, bulk_recv, base_send, base_recv, trace_send, trace_recv,
-    ready_sem,
+    ready_sem, near_sem, relay_send, relay_recv, passed,
 ):
     shots, rows, _, planes, width = held.shape
     half = shots // 2
@@ -52,6 +55,15 @@
     has_above = d > 0
     has_below = d < layers - 1
     inner = has_above & has_below
+    seam_prev = has_prev & (l % RING == 0)
+    seam_next = has_next & (l % RING == RING - 1)
+    seam = seam_prev | seam_next
+    at_pair = l % (2 * RING)
+
+    def seam_at(tile):
+        at = tile % RING
+        return ((tile > 0) & (at == 0)) | ((tile < tiles - 1) & (at == RING - 1))
+
     side_one = jnp.where(d >= layers // 2, 1, 0)
     side_two = 1 - side_one
 
@@ -68,14 +80,22 @@
         )
     ]
     barrier = pltpu.get_barrier_semaphore()
-    beside = ((has_prev, 0, -1), (has_next, 0, 1), (has_above, -1, 0), (has_below, 1, 0))
-    for there, by_d, by_l in beside:
+    for there, by_d, by_l in (
+        (has_prev & (seam | jnp.logical_not(seam_at(l - 1))), 0, -1),
+        (has_next & (seam | jnp.logical_not(seam_at(l + 1))), 0, 1),
+        (has_above & jnp.logical_not(seam), -1, 0),
+        (has_below & jnp.logical_not(seam), 1, 0),
+        ((at_pair == 5) & (l > 5), 0, -7),
+        ((at_pair == 2) & (l + 6 < tiles), 0, 7),
+    ):
 
         @pl.when(there)
         def _():
             pl.semaphore_signal(barrier, inc=1, device_id=(d + by_d, l + by_l), device_id_type=MESH)
 
-    expected = sum(jnp.where(there, 1, 0) for there, _, _ in beside)
+    layers_beside = jnp.where(has_above, 1, 0) + jnp.where(has_below, 1, 0)
+    tiles_beside = jnp.where(has_prev, 1, 0) + jnp.where(has_next, 1, 0)
+    tiles_beyond = jnp.where(((at_pair == 6) & (l + 2 < tiles)) | ((at_pair == 1) & (l > 1)), 1, 0)
 
     small[0].start()
     for r in (0, 3, 1, 2):
@@ -159,25 +179,54 @@
             )
             base[side, part, r + 2, pl.ds(s % half, 1), :] = row
 
-    def piece(k, to_next):
+    cut = planes - RELAY
+
+    def piece(k, to_next, stop=planes):
         s, a, part = k // 4, (k % 4) // 2, k % 2
-        if to_next:
-            return pltpu.make_async_remote_copy(
-                src_ref=solved.at[s, 3 - a, part],
-                dst_ref=halo.at[s, 1 - a, part],
-                send_sem=bulk_send.at[1, k],
-                recv_sem=bulk_recv.at[1, k],
-                device_id=(d, l + 1),
-                device_id_type=MESH,
-            )
+        row, at = (3 - a, 1 - a) if to_next else (a, 2 + a)
         return pltpu.make_async_remote_copy(
-            src_ref=solved.at[s, a, part],
-            dst_ref=halo.at[s, 2 + a, part],
-            send_sem=bulk_send.at[0, k],
-            recv_sem=bulk_recv.at[0, k],
-            device_id=(d, l - 1),
+            src_ref=solved.at[s, row, part, pl.ds(0, stop)],
+            dst_ref=halo.at[s, at, part, pl.ds(0, stop)],
+            send_sem=bulk_send.at[int(to_next), k],
+            recv_sem=bulk_recv.at[int(to_next), k],
+            device_id=(d, l + 1 if to_next else l - 1),
             device_id_type=MESH,
         )
+
+    relays = (
+        (0, 0, (at_pair == 3) | ((at_pair == 7) & has_next), -1),
+        (0, 1, (at_pair == 2) | ((at_pair == 6) & (l + 2 < tiles)), jnp.where(at_pair == 6, 7, -1)),
+        (0, 2, (at_pair == 1) | ((at_pair == 5) & (l > 5)), jnp.where(at_pair == 5, -5, 3)),
+        (1, 0, (at_pair == 4) | ((at_pair == 0) & has_prev), 1),
+        (1, 1, (at_pair == 5) | ((at_pair == 1) & (l > 1)), jnp.where(at_pair == 1, -7, 1)),
+        (1, 2, (at_pair == 6) | ((at_pair == 2) & (l + 6 < tiles)), jnp.where(at_pair == 2, 5, -3)),
+    )
+    relay_by = {(way, stage): by for way, stage, _, by in relays}
+
+    def relay(way, stage):
+        if stage == 0:
+            kept = solved.at[0, 0 if way else rows - 1, 0, pl.ds(cut, RELAY)]
+        else:
+            kept = passed.at[way, stage - 1]
+        there = halo.at[0, 2 if way else 1, 0, pl.ds(cut, RELAY)] if stage == 2 else passed.at[way, stage]
+        return pltpu.make_async_remote_copy(
+            src_ref=kept,
+            dst_ref=there,
+            send_sem=relay_send.at[way, stage],
+            recv_sem=relay_recv.at[way, stage],
+            device_id=(d, l + relay_by[way, stage]),
+            device_id_type=MESH,
+        )
+
+    def relay_on(stage):
+        for way, at, here, _ in relays:
+            if at == stage:
+
+                @pl.when(here)
+                def _():
+                    if stage > 0:
+                        relay(way, stage - 1).wait_recv()
+                    relay(way, stage).start()
 
     def send_pieces(start, stop):
         for to_next, there in ((False, has_prev), (True, has_next)):
@@ -190,16 +239,52 @@
 
                 lax.fori_loop(start, stop, step, 0)
 
+    def send_first(to_next, there, stop):
+        @pl.when(there)
+        def _():
+            piece(0, to_next, stop).start()
+            for k in range(1, PIECES_FIRST):
+                piece(k, to_next).start()
+
     solve(0, 0)
     solve(0, 3)
-    pl.semaphore_wait(barrier, expected)
-    send_pieces(0, PIECES_FIRST)
-    for there, by_d in ((has_above, -1), (has_below, 1)):
-
-        @pl.when(there)
-        def _():
-            pl.semaphore_signal(ready_sem, inc=1, device_id=(d + by_d, l), device_id_type=MESH)
-
+
+    def tell_layers():
+        for there, by_d in ((has_above, -1), (has_below, 1)):
+
+            @pl.when(there)
+            def _():
+                pl.semaphore_signal(ready_sem, inc=1, device_id=(d + by_d, l), device_id_type=MESH)
+
+    @pl.when(jnp.logical_not(seam))
+    def _():
+        pl.semaphore_wait(barrier, tiles_beside + tiles_beyond + layers_beside)
+        for there, by_l in ((has_prev & seam_at(l - 1), -1), (has_next & seam_at(l + 1), 1)):
+
+            @pl.when(there)
+            def _():
+                pl.semaphore_signal(near_sem, inc=1, device_id=(d, l + by_l), device_id_type=MESH)
+
+    @pl.when(seam)
+    def _():
+        pl.semaphore_wait(near_sem, 1)
+
+    near_prev = has_prev & jnp.logical_not(seam_prev)
+    near_next = has_next & jnp.logical_not(seam_next)
+    send_first(False, near_prev, planes)
+    send_first(True, near_next, planes)
+
+    @pl.when(jnp.logical_not(seam))
+    def _():
+        tell_layers()
+
+    @pl.when(seam)
+    def _():
+        pl.semaphore_wait(barrier, 1)
+
+    send_first(False, seam_prev, cut)
+    send_first(True, seam_next, cut)
+    relay_on(0)
     solve(0, 1)
     solve(0, 2)
     send_pieces(PIECES_FIRST, PIECES_SOLVE)
@@ -230,6 +315,10 @@
 
     def both(needed, there):
         return there if needed is True else needed & there
+
+    @pl.when(jnp.logical_not(seam))
+    def _():
+        pl.semaphore_wait(ready_sem, layers_beside)
 
     for needed, to_next, side in base_copies:
 
@@ -276,7 +365,12 @@
         def _():
             base_copy(side, to_next).wait_recv()
 
-    pl.semaphore_wait(ready_sem, jnp.where(has_above, 1, 0) + jnp.where(has_below, 1, 0))
+    @pl.when(seam)
+    def _():
+        tell_layers()
+        pl.semaphore_wait(ready_sem, layers_beside)
+
+    relay_on(1)
 
     def lateral(values, r):
         at = r + 2
@@ -368,14 +462,23 @@
 
     @pl.when(jnp.logical_not(inner))
     def _():
-        send_pieces(PIECES_SOLVE + PIECES_BASE_OUTER, pieces)
+        send_pieces(PIECES_SOLVE + PIECES_BASE_OUTER, pieces - HELD_BACK)
 
     take(side_two)
 
     @pl.when(inner)
     def _():
         emit(side_two)
+
+    relay_on(2)
+
+    @pl.when(inner)
+    def _():
         send_pieces(sent_inner + PIECES_TRACE, pieces)
+
+    @pl.when(jnp.logical_not(inner))
+    def _():
+        send_pieces(pieces - HELD_BACK, pieces)
 
     for side in range(2):
         for part in range(2):
@@ -418,9 +521,9 @@
 
     lax.fori_loop(0, shots, own_rows, 0)
 
-    def add_rows(s, part, q, to_rows):
-        for first in range(0, planes, BLOCK):
-            at = pl.ds(first, BLOCK)
+    def add_rows(s, part, q, to_rows, start=0, stop=planes):
+        for first in range(start, stop, BLOCK):
+            at = pl.ds(first, min(BLOCK, stop - first))
             v = halo[s, q, part, at, :]
             for r, weight in to_rows:
                 field[s, r, part, at, :] = field[s, r, part, at, :] + (CORRECTION * weight) * v
@@ -439,25 +542,56 @@
         for goes, _, copy in trace_copies(side_two):
             under(goes, lambda: copy().wait_send())
 
+    from_next = (((3, NEAR), (2, FAR)), ((3, FAR),))
+    from_prev = (((0, NEAR), (1, FAR)), ((0, FAR),))
+
+    def add_piece(s, a, part, stop_prev, stop_next):
+        k = s * 4 + a * 2 + part
+        for there, to_next, stop, q, to_rows in (
+            (has_next, True, stop_next, 2 + a, from_next[a]),
+            (has_prev, False, stop_prev, 1 - a, from_prev[a]),
+        ):
+
+            @pl.when(there)
+            def _():
+                piece(k, not to_next, stop).wait_recv()
+                piece(k, to_next, stop).wait_send()
+                add_rows(s, part, q, to_rows, 0, stop)
+
     def add_shot(s, carry):
         for a in range(2):
             for part in range(2):
-                k = s * 4 + a * 2 + part
-
-                @pl.when(has_next)
-                def _():
-                    piece(k, False).wait_recv()
-                    piece(k, True).wait_send()
-                    add_rows(s, part, 2 + a, ((3, NEAR), (2, FAR)) if a == 0 else ((3, FAR),))
-
-                @pl.when(has_prev)
-                def _():
-                    piece(k, True).wait_recv()
-                    piece(k, False).wait_send()
-                    add_rows(s, part, 1 - a, ((0, NEAR), (1, FAR)) if a == 0 else ((0, FAR),))
+                add_piece(s, a, part, planes, planes)
         return carry
 
-    lax.fori_loop(0, shots, add_shot, 0)
+    def add_first(to_next, there, stop):
+        @pl.when(there)
+        def _():
+            piece(0, not to_next, stop).wait_recv()
+            piece(0, to_next, stop).wait_send()
+            add_rows(0, 0, 2 if to_next else 1, (from_next if to_next else from_prev)[0], 0, stop)
+
+    add_first(True, near_next, planes)
+    add_first(False, near_prev, planes)
+    add_first(True, seam_next, cut)
+    add_first(False, seam_prev, cut)
+    for a, part in ((0, 1), (1, 0), (1, 1)):
+        add_piece(0, a, part, planes, planes)
+    lax.fori_loop(1, shots - 1, add_shot, 0)
+    for way, stage, here, _ in relays:
+
+        @pl.when(here)
+        def _():
+            relay(way, stage).wait_send()
+
+    for to_next, there in ((True, seam_next), (False, seam_prev)):
+
+        @pl.when(there)
+        def _():
+            relay(1 if to_next else 0, 2).wait_recv()
+            add_rows(0, 0, 2 if to_next else 1, (from_next if to_next else from_prev)[0], cut, planes)
+
+    add_shot(shots - 1, 0)
 
 
 def write_kernel(field, out, sem):
@@ -517,6 +651,10 @@
             dma((2, 3)),
             dma((2, 3)),
             pltpu.SemaphoreType.REGULAR,
+            pltpu.SemaphoreType.REGULAR,
+            dma((2, 3)),
+            dma((2, 3)),
+            pltpu.VMEM((2, 2, RELAY, width), jnp.float32),
         ],
         compiler_params=pltpu.CompilerParams(
             collective_id=0, has_side_effects=True, vmem_limit_bytes=40 * 2**20

time: 69.8 us -> 68.5 us (0.981)
  Pallas kernels: 69 us -> 67.8 us
    pallas_call x1, Pallas kernels: 66.5 us -> 65.3 us  [on_device(): pl.pallas_call(field_kernel, out_shape=jax.ShapeDtypeStruct(by_rows, jnp....]
where the time goes in v3:
time: 68.5 us; the launch traced here: 68.4 us
  Pallas kernels  67.8 us (99%)
    pallas_call x1, Pallas kernels, on_device(): pl.pallas_call(field_kernel, out_shape=jax.ShapeDtypeStruct(by_rows, jnp....  65.3 us
    pallas_call x1, Pallas kernels, on_device(): pl.pallas_call(write_kernel, out_shape=jax.ShapeDtypeStruct(source.shape,...  2.46 us

profile of v3, /device:TPU:97, one launch (start us, length us, event | category | flops | bytes accessed | tf_op | source)
XLA Modules:
  0.0 68.4 jit_solution(17103602669912349236)
XLA Ops:
  0.7 65.3 %shard_map.64.field = f32[4,4,2,80,512]{4,3,2,1,0:T(8,128)S(1)} custom-call(s32[1]{0:T(128)S(6)} %copy.7.count, f32[4,2,80,4,512]{4,3,2,1,0:T(4,128)} %source.1, f32[1,2,80,80]{3,2,1,0:T(8,128)} %matrix_from.1, s32[80,4,512]{2,1,0:T(4,128)} %classes.1, f32[16]{0:T(128)} %table_re_from.1, f32[16]{0:T(128)} %table_im_from.1), custom_call_target="tpu_custom_call" | custom-call | tf_op jit(solution)/shard_map/pallas_call | solution.py:622
  65.9 2.5 %shard_map.65 = f32[4,2,80,4,512]{4,3,2,1,0:T(4,128)} custom-call(f32[4,4,2,80,512]{4,3,2,1,0:T(8,128)S(1)} %shard_map.64.field), custom_call_target="tpu_custom_call" | custom-call | tf_op jit(solution)/shard_map/pallas_call | solution.py:663

commit v4 on v3

--- a/solution.py
+++ b/solution.py
@@ -15,13 +15,25 @@
 BLOCK = 16
 EXTRA = 16
 RING = 4
-RELAY = 40
-HELD_BACK = 4
-PIECES_FIRST = 2
-PIECES_SOLVE = 3
-PIECES_BASE_OUTER = 2
-PIECES_BASE_INNER = 4
-PIECES_TRACE = 3
+RELAY = 48
+PIECES = (
+    (0, 0, 1, 0, 1),
+    (0, 0, 1, 1, 1),
+    (0, 1, 1, 0, 1),
+    (0, 1, 1, 1, 1),
+    (1, 0, 1, 0, 2),
+    (1, 1, 1, 0, 2),
+    (2, 0, 2, 0, 2),
+    (3, 0, 1, 0, 2),
+    (3, 1, 1, 0, 1),
+    (3, 1, 1, 1, 1),
+)
+AFTER_FIRST = 2
+AFTER_SHOT = 3
+AFTER_BASE_OUTER = 5
+AFTER_BASE_INNER = 5
+AFTER_TRACE_INNER = 6
+AFTER_TRACE_OUTER = 7
 
 
 def along_y(x):
@@ -45,7 +57,6 @@
 ):
     shots, rows, _, planes, width = held.shape
     half = shots // 2
-    pieces = shots * 4
     d = lax.axis_index("depth")
     l = lax.axis_index("lat")
     layers = lax.axis_size("depth")
@@ -182,11 +193,11 @@
     cut = planes - RELAY
 
     def piece(k, to_next, stop=planes):
-        s, a, part = k // 4, (k % 4) // 2, k % 2
-        row, at = (3 - a, 1 - a) if to_next else (a, 2 + a)
+        s, a, count_rows, part, parts = PIECES[k]
+        row, at = (rows - a - count_rows, 2 - a - count_rows) if to_next else (a, 2 + a)
         return pltpu.make_async_remote_copy(
-            src_ref=solved.at[s, row, part, pl.ds(0, stop)],
-            dst_ref=halo.at[s, at, part, pl.ds(0, stop)],
+            src_ref=solved.at[s, pl.ds(row, count_rows), pl.ds(part, parts), pl.ds(0, stop)],
+            dst_ref=halo.at[s, pl.ds(at, count_rows), pl.ds(part, parts), pl.ds(0, stop)],
             send_sem=bulk_send.at[int(to_next), k],
             recv_sem=bulk_recv.at[int(to_next), k],
             device_id=(d, l + 1 if to_next else l - 1),
@@ -233,17 +244,14 @@
 
             @pl.when(there)
             def _():
-                def step(k, carry):
+                for k in range(start, stop):
                     piece(k, to_next).start()
-                    return carry
-
-                lax.fori_loop(start, stop, step, 0)
 
     def send_first(to_next, there, stop):
         @pl.when(there)
         def _():
             piece(0, to_next, stop).start()
-            for k in range(1, PIECES_FIRST):
+            for k in range(1, AFTER_FIRST):
                 piece(k, to_next).start()
 
     solve(0, 0)
@@ -287,7 +295,7 @@
     relay_on(0)
     solve(0, 1)
     solve(0, 2)
-    send_pieces(PIECES_FIRST, PIECES_SOLVE)
+    send_pieces(AFTER_FIRST, AFTER_SHOT)
 
     def solve_shot(s, carry):
         for r in range(rows):
@@ -328,11 +336,11 @@
 
     @pl.when(inner)
     def _():
-        send_pieces(PIECES_SOLVE, PIECES_SOLVE + PIECES_BASE_INNER)
+        send_pieces(AFTER_SHOT, AFTER_BASE_INNER)
 
     @pl.when(jnp.logical_not(inner))
     def _():
-        send_pieces(PIECES_SOLVE, PIECES_SOLVE + PIECES_BASE_OUTER)
+        send_pieces(AFTER_SHOT, AFTER_BASE_OUTER)
 
     small[1].wait()
     small[2].wait()
@@ -454,15 +462,14 @@
         take(side_one)
 
     emit(side_one)
-    sent_inner = PIECES_SOLVE + PIECES_BASE_INNER
 
     @pl.when(inner)
     def _():
-        send_pieces(sent_inner, sent_inner + PIECES_TRACE)
+        send_pieces(AFTER_BASE_INNER, AFTER_TRACE_INNER)
 
     @pl.when(jnp.logical_not(inner))
     def _():
-        send_pieces(PIECES_SOLVE + PIECES_BASE_OUTER, pieces - HELD_BACK)
+        send_pieces(AFTER_BASE_OUTER, AFTER_TRACE_OUTER)
 
     take(side_two)
 
@@ -474,11 +481,11 @@
 
     @pl.when(inner)
     def _():
-        send_pieces(sent_inner + PIECES_TRACE, pieces)
+        send_pieces(AFTER_TRACE_INNER, len(PIECES))
 
     @pl.when(jnp.logical_not(inner))
     def _():
-        send_pieces(pieces - HELD_BACK, pieces)
+        send_pieces(AFTER_TRACE_OUTER, len(PIECES))
 
     for side in range(2):
         for part in range(2):
@@ -545,39 +552,32 @@
     from_next = (((3, NEAR), (2, FAR)), ((3, FAR),))
     from_prev = (((0, NEAR), (1, FAR)), ((0, FAR),))
 
-    def add_piece(s, a, part, stop_prev, stop_next):
-        k = s * 4 + a * 2 + part
-        for there, to_next, stop, q, to_rows in (
-            (has_next, True, stop_next, 2 + a, from_next[a]),
-            (has_prev, False, stop_prev, 1 - a, from_prev[a]),
-        ):
-
-            @pl.when(there)
-            def _():
-                piece(k, not to_next, stop).wait_recv()
-                piece(k, to_next, stop).wait_send()
-                add_rows(s, part, q, to_rows, 0, stop)
-
-    def add_shot(s, carry):
-        for a in range(2):
-            for part in range(2):
-                add_piece(s, a, part, planes, planes)
-        return carry
-
-    def add_first(to_next, there, stop):
+    def add_piece(k, to_next, there, stop=planes):
+        s, first_row, count_rows, first_part, parts = PIECES[k]
+
         @pl.when(there)
         def _():
-            piece(0, not to_next, stop).wait_recv()
-            piece(0, to_next, stop).wait_send()
-            add_rows(0, 0, 2 if to_next else 1, (from_next if to_next else from_prev)[0], 0, stop)
-
-    add_first(True, near_next, planes)
-    add_first(False, near_prev, planes)
-    add_first(True, seam_next, cut)
-    add_first(False, seam_prev, cut)
-    for a, part in ((0, 1), (1, 0), (1, 1)):
-        add_piece(0, a, part, planes, planes)
-    lax.fori_loop(1, shots - 1, add_shot, 0)
+            piece(k, not to_next, stop).wait_recv()
+            piece(k, to_next, stop).wait_send()
+            for a in range(first_row, first_row + count_rows):
+                q, to_rows = (2 + a, from_next[a]) if to_next else (1 - a, from_prev[a])
+
+                def add_part(part, carry):
+                    add_rows(s, part, q, to_rows, 0, stop)
+                    return carry
+
+                if parts == 1:
+                    add_part(first_part, 0)
+                else:
+                    lax.fori_loop(first_part, first_part + parts, add_part, 0)
+
+    add_piece(0, True, near_next)
+    add_piece(0, False, near_prev)
+    add_piece(0, True, seam_next, cut)
+    add_piece(0, False, seam_prev, cut)
+    for k in range(1, AFTER_TRACE_INNER):
+        add_piece(k, True, has_next)
+        add_piece(k, False, has_prev)
     for way, stage, here, _ in relays:
 
         @pl.when(here)
@@ -591,7 +591,9 @@
             relay(1 if to_next else 0, 2).wait_recv()
             add_rows(0, 0, 2 if to_next else 1, (from_next if to_next else from_prev)[0], cut, planes)
 
-    add_shot(shots - 1, 0)
+    for k in range(AFTER_TRACE_INNER, len(PIECES)):
+        add_piece(k, True, has_next)
+        add_piece(k, False, has_prev)
 
 
 def write_kernel(field, out, sem):
@@ -616,7 +618,7 @@
     hbm = pl.BlockSpec(memory_space=pltpu.HBM)
     vmem = pl.BlockSpec(memory_space=pltpu.VMEM)
     tall = 2 * planes + EXTRA
-    pieces = shots * 4
+    pieces = len(PIECES)
     dma = pltpu.SemaphoreType.DMA
     operands = (source, line_inverse, classes, table_re, table_im)
     field = pl.pallas_call(

time: 68.5 us -> 67.9 us (level)
  Pallas kernels: 67.8 us -> 67.1 us
where the time goes in v4:
time: 67.9 us; the launch traced here: 67.8 us
  Pallas kernels  67.1 us (99%)
    pallas_call x1, Pallas kernels, on_device(): pl.pallas_call(field_kernel, out_shape=jax.ShapeDtypeStruct(by_rows, jnp....  64.7 us
    pallas_call x1, Pallas kernels, on_device(): pl.pallas_call(write_kernel, out_shape=jax.ShapeDtypeStruct(source.shape,...  2.46 us

profile of v4, /device:TPU:97, one launch (start us, length us, event | category | flops | bytes accessed | tf_op | source)
XLA Modules:
  0.0 67.8 jit_solution(7518397866928399518)
XLA Ops:
  0.7 64.7 %shard_map.64.field = f32[4,4,2,80,512]{4,3,2,1,0:T(8,128)S(1)} custom-call(s32[1]{0:T(128)S(6)} %copy.7.count, f32[4,2,80,4,512]{4,3,2,1,0:T(4,128)} %source.1, f32[1,2,80,80]{3,2,1,0:T(8,128)} %matrix_from.1, s32[80,4,512]{2,1,0:T(4,128)} %classes.1, f32[16]{0:T(128)} %table_re_from.1, f32[16]{0:T(128)} %table_im_from.1), custom_call_target="tpu_custom_call" | custom-call | tf_op jit(solution)/shard_map/pallas_call | solution.py:624
  65.3 2.5 %shard_map.65 = f32[4,2,80,4,512]{4,3,2,1,0:T(4,128)} custom-call(f32[4,4,2,80,512]{4,3,2,1,0:T(8,128)S(1)} %shard_map.64.field), custom_call_target="tpu_custom_call" | custom-call | tf_op jit(solution)/shard_map/pallas_call | solution.py:665

commit v5 on v4

--- a/solution.py
+++ b/solution.py
@@ -19,10 +19,8 @@
 PIECES = (
     (0, 0, 1, 0, 1),
     (0, 0, 1, 1, 1),
-    (0, 1, 1, 0, 1),
-    (0, 1, 1, 1, 1),
-    (1, 0, 1, 0, 2),
-    (1, 1, 1, 0, 2),
+    (0, 1, 1, 0, 2),
+    (1, 0, 2, 0, 2),
     (2, 0, 2, 0, 2),
     (3, 0, 1, 0, 2),
     (3, 1, 1, 0, 1),
@@ -30,10 +28,10 @@
 )
 AFTER_FIRST = 2
 AFTER_SHOT = 3
-AFTER_BASE_OUTER = 5
-AFTER_BASE_INNER = 5
-AFTER_TRACE_INNER = 6
-AFTER_TRACE_OUTER = 7
+AFTER_BASE_OUTER = 3
+AFTER_BASE_INNER = 4
+AFTER_TRACE_INNER = 4
+AFTER_TRACE_OUTER = 5
 
 
 def along_y(x):

time: 67.9 us -> 67.8 us (level)
  no operation moved by 1% of the time
where the time goes in v5:
time: 67.8 us; the launch traced here: 67.7 us
  Pallas kernels  67.1 us (99%)
    pallas_call x1, Pallas kernels, on_device(): pl.pallas_call(field_kernel, out_shape=jax.ShapeDtypeStruct(by_rows, jnp....  64.6 us
    pallas_call x1, Pallas kernels, on_device(): pl.pallas_call(write_kernel, out_shape=jax.ShapeDtypeStruct(source.shape,...  2.46 us

profile of v5, /device:TPU:97, one launch (start us, length us, event | category | flops | bytes accessed | tf_op | source)
XLA Modules:
  0.0 67.7 jit_solution(7101012002244974318)
XLA Ops:
  0.7 64.6 %shard_map.64.field = f32[4,4,2,80,512]{4,3,2,1,0:T(8,128)S(1)} custom-call(s32[1]{0:T(128)S(6)} %copy.7.count, f32[4,2,80,4,512]{4,3,2,1,0:T(4,128)} %source.1, f32[1,2,80,80]{3,2,1,0:T(8,128)} %matrix_from.1, s32[80,4,512]{2,1,0:T(4,128)} %classes.1, f32[16]{0:T(128)} %table_re_from.1, f32[16]{0:T(128)} %table_im_from.1), custom_call_target="tpu_custom_call" | custom-call | tf_op jit(solution)/shard_map/pallas_call | solution.py:622
  65.3 2.5 %shard_map.65 = f32[4,2,80,4,512]{4,3,2,1,0:T(4,128)} custom-call(f32[4,4,2,80,512]{4,3,2,1,0:T(8,128)S(1)} %shard_map.64.field), custom_call_target="tpu_custom_call" | custom-call | tf_op jit(solution)/shard_map/pallas_call | solution.py:663

commit v6 on v5

--- a/solution.py
+++ b/solution.py
@@ -31,7 +31,7 @@
 AFTER_BASE_OUTER = 3
 AFTER_BASE_INNER = 4
 AFTER_TRACE_INNER = 4
-AFTER_TRACE_OUTER = 5
+AFTER_TRACE_OUTER = 6
 
 
 def along_y(x):

time: 67.8 us -> 67.8 us (level)
  no operation moved by 1% of the time
where the time goes in v6:
time: 67.8 us; the launch traced here: 67.7 us
  Pallas kernels  67.1 us (99%)
    pallas_call x1, Pallas kernels, on_device(): pl.pallas_call(field_kernel, out_shape=jax.ShapeDtypeStruct(by_rows, jnp....  64.6 us
    pallas_call x1, Pallas kernels, on_device(): pl.pallas_call(write_kernel, out_shape=jax.ShapeDtypeStruct(source.shape,...  2.46 us

profile of v6, /device:TPU:97, one launch (start us, length us, event | category | flops | bytes accessed | tf_op | source)
XLA Modules:
  0.0 67.7 jit_solution(12896924098688105802)
XLA Ops:
  0.7 64.6 %shard_map.64.field = f32[4,4,2,80,512]{4,3,2,1,0:T(8,128)S(1)} custom-call(s32[1]{0:T(128)S(6)} %copy.7.count, f32[4,2,80,4,512]{4,3,2,1,0:T(4,128)} %source.1, f32[1,2,80,80]{3,2,1,0:T(8,128)} %matrix_from.1, s32[80,4,512]{2,1,0:T(4,128)} %classes.1, f32[16]{0:T(128)} %table_re_from.1, f32[16]{0:T(128)} %table_im_from.1), custom_call_target="tpu_custom_call" | custom-call | tf_op jit(solution)/shard_map/pallas_call | solution.py:622
  65.3 2.5 %shard_map.65 = f32[4,2,80,4,512]{4,3,2,1,0:T(4,128)} custom-call(f32[4,4,2,80,512]{4,3,2,1,0:T(8,128)S(1)} %shard_map.64.field), custom_call_target="tpu_custom_call" | custom-call | tf_op jit(solution)/shard_map/pallas_call | solution.py:663

commit v7 on v6

--- a/solution.py
+++ b/solution.py
@@ -23,8 +23,7 @@
     (1, 0, 2, 0, 2),
     (2, 0, 2, 0, 2),
     (3, 0, 1, 0, 2),
-    (3, 1, 1, 0, 1),
-    (3, 1, 1, 1, 1),
+    (3, 1, 1, 0, 2),
 )
 AFTER_FIRST = 2
 AFTER_SHOT = 3

time: 67.8 us -> 67.8 us (level)
  no operation moved by 1% of the time
where the time goes in v7:
time: 67.8 us; the launch traced here: 67.7 us
  Pallas kernels  67 us (99%)
    pallas_call x1, Pallas kernels, on_device(): pl.pallas_call(field_kernel, out_shape=jax.ShapeDtypeStruct(by_rows, jnp....  64.6 us
    pallas_call x1, Pallas kernels, on_device(): pl.pallas_call(write_kernel, out_shape=jax.ShapeDtypeStruct(source.shape,...  2.46 us

profile of v7, /device:TPU:97, one launch (start us, length us, event | category | flops | bytes accessed | tf_op | source)
XLA Modules:
  0.0 67.7 jit_solution(18188561260661778920)
XLA Ops:
  0.7 64.6 %shard_map.64.field = f32[4,4,2,80,512]{4,3,2,1,0:T(8,128)S(1)} custom-call(s32[1]{0:T(128)S(6)} %copy.7.count, f32[4,2,80,4,512]{4,3,2,1,0:T(4,128)} %source.1, f32[1,2,80,80]{3,2,1,0:T(8,128)} %matrix_from.1, s32[80,4,512]{2,1,0:T(4,128)} %classes.1, f32[16]{0:T(128)} %table_re_from.1, f32[16]{0:T(128)} %table_im_from.1), custom_call_target="tpu_custom_call" | custom-call | tf_op jit(solution)/shard_map/pallas_call | solution.py:621
  65.2 2.5 %shard_map.65 = f32[4,2,80,4,512]{4,3,2,1,0:T(4,128)} custom-call(f32[4,4,2,80,512]{4,3,2,1,0:T(8,128)S(1)} %shard_map.64.field), custom_call_target="tpu_custom_call" | custom-call | tf_op jit(solution)/shard_map/pallas_call | solution.py:662
